TPU v7x, 32 devices: a whole 2x2x4 slice. The times are simulated.
32 devices in a mesh: cuts: 4 (over x, core), exp: 2 (over y), fsdp: 4 (over z).
Axes of the slice: x: 2, y: 2, z: 4, core: 2. Of those that a mesh axis runs over, the one named last changes fastest.
Arguments:
- tokens: bfloat16 [4096, 4096], P(('cuts', 'exp', 'fsdp')), may hold values from -6 to 6
- out_grad: bfloat16 [4096, 4096], P(('cuts', 'exp', 'fsdp')), may hold values from -6 to 6
- expert_ids: int32 [4096, 2], P(('cuts', 'exp', 'fsdp')), may hold values from 0 to 7, as said below
- gate_probs: bfloat16 [4096, 2], P(('cuts', 'exp', 'fsdp')), may hold values from 0.049804688 to 0.94921875
- params: float32 [3, 8, 4096, 256], P(None, 'exp', ('cuts', 'fsdp')), may hold values from -0.1875 to 0.1875
- moment_first: float32 [3, 8, 4096, 256], P(None, 'exp', ('cuts', 'fsdp')), may hold values from -60 to 60
- moment_second: float32 [3, 8, 4096, 256], P(None, 'exp', ('cuts', 'fsdp')), may hold values from 64 to 1024
Outputs:
- token_grad: bfloat16 [4096, 4096], P(('cuts', 'exp', 'fsdp'))
- gate_grad: bfloat16 [4096, 2], P(('cuts', 'exp', 'fsdp'))
- new_params: float32 [3, 8, 4096, 256], P(None, 'exp', ('cuts', 'fsdp'))
- new_first: float32 [3, 8, 4096, 256], P(None, 'exp', ('cuts', 'fsdp'))
- new_second: float32 [3, 8, 4096, 256], P(None, 'exp', ('cuts', 'fsdp'))
Inputs may be any that keep to these rules, and one draw needn't show every extreme that they name: `expert_ids`: the two ids of a token differ. Among the tokens of one device no expert is named more than 40 times. Each device names some expert exactly 40 times, and the devices that share their cuts and fsdp indices have one such expert in common.
All inputs are finite; a program needn't handle non-finite values.
Results may differ from a plain program's by a relative error of at most 0.0079.
Values may be sent and summed in bfloat16 or wider, within the bound.
A program may use at most 192 MiB of HBM per device.

v0:
```python
import jax
import jax.numpy as jnp
from jax import lax
from jax.sharding import PartitionSpec as P

EXPERTS = 8
decay_first = 0.9
decay_second = 0.95
correct_first = 1.0 - 0.9**10
correct_second = 1.0 - 0.95**10
epsilon = 1e-08
learn_rate = 0.0003
weight_decay = 0.1


def adam_update(params, gradient, moment_first, moment_second):
    new_first = decay_first * moment_first + (1.0 - decay_first) * gradient
    new_second = decay_second * moment_second + (1.0 - decay_second) * gradient * gradient
    stepped = new_first / correct_first / (jnp.sqrt(new_second / correct_second) + epsilon)
    new_params = params - learn_rate * (stepped + weight_decay * params)
    return (new_params, new_first, new_second)


def per_device(tokens, out_grad, expert_ids, gate_probs, params, moment_first, moment_second):
    token_count = tokens.shape[0]
    width = tokens.shape[1]
    local_count = params.shape[1]
    exp_count = lax.axis_size("exp")
    capacity = 10 * token_count // 32
    weights = lax.all_gather(params.astype(jnp.bfloat16), ("cuts", "fsdp"), axis=2, tiled=True)
    flat_ids = expert_ids.reshape(-1)
    onehot = (flat_ids[:, None] == jnp.arange(EXPERTS, dtype=jnp.int32)[None, :]).astype(jnp.int32)
    before = jnp.cumsum(onehot, axis=0) - onehot
    position = jnp.sum(before * onehot, axis=1)
    holder = flat_ids // local_count
    local_index = flat_ids % local_count
    target = (local_index * exp_count + holder) * capacity + position
    placement = (
        target[:, None] == jnp.arange(EXPERTS * capacity, dtype=jnp.int32)[None, :]
    ).astype(jnp.bfloat16)
    token_place = jnp.sum(placement.reshape(token_count, 2, EXPERTS * capacity), axis=1)
    send_inputs = jnp.einsum(
        "tc,td->cd", token_place, tokens, preferred_element_type=jnp.float32
    ).astype(jnp.bfloat16)
    send_upstream = jnp.einsum(
        "tc,td->cd", token_place, out_grad, preferred_element_type=jnp.float32
    ).astype(jnp.bfloat16)
    send_gates = jnp.einsum(
        "pc,p->c", placement, gate_probs.reshape(-1), preferred_element_type=jnp.float32
    ).astype(jnp.bfloat16)
    layout = (local_count, exp_count, capacity)
    arrived_inputs, arrived_upstream, arrived_gates = (
        lax.all_to_all(
            send_inputs.reshape(layout + (width,)), "exp", split_axis=1, concat_axis=1, tiled=True
        ),
        lax.all_to_all(
            send_upstream.reshape(layout + (width,)), "exp", split_axis=1, concat_axis=1, tiled=True
        ),
        lax.all_to_all(
            send_gates.reshape(layout + (1,)), "exp", split_axis=1, concat_axis=1, tiled=True
        ),
    )
    slot_count = exp_count * capacity
    arrived_inputs = arrived_inputs.reshape(local_count, slot_count, width)
    arrived_upstream = arrived_upstream.reshape(local_count, slot_count, width)
    gate_values = arrived_gates.reshape(local_count, slot_count, 1).astype(jnp.float32)
    w_gate = weights[0]
    w_up = weights[1]
    w_down = weights[2]
    pre_gate = jnp.einsum(
        "esd,edf->esf", arrived_inputs, w_gate, preferred_element_type=jnp.float32
    )
    pre_up = jnp.einsum("esd,edf->esf", arrived_inputs, w_up, preferred_element_type=jnp.float32)
    sigmoid_gate = jax.nn.sigmoid(pre_gate)
    activated = pre_gate * sigmoid_gate
    hidden = activated * pre_up
    projected = jnp.einsum(
        "esd,edf->esf", arrived_upstream, w_down, preferred_element_type=jnp.float32
    )
    slot_gate = jnp.sum(hidden * projected, axis=2, keepdims=True).astype(jnp.bfloat16)
    delta_hidden = gate_values * projected
    delta_gate = (
        delta_hidden * pre_up * sigmoid_gate * (1.0 + pre_gate * (1.0 - sigmoid_gate))
    ).astype(jnp.bfloat16)
    delta_up = (delta_hidden * activated).astype(jnp.bfloat16)
    scaled = (gate_values * arrived_upstream.astype(jnp.float32)).astype(jnp.bfloat16)
    slot_grads = (
        jnp.einsum("esf,edf->esd", delta_gate, w_gate, preferred_element_type=jnp.float32)
        + jnp.einsum("esf,edf->esd", delta_up, w_up, preferred_element_type=jnp.float32)
    ).astype(jnp.bfloat16)
    returned_grads, returned_gate = (
        lax.all_to_all(
            slot_grads.reshape(layout + (width,)), "exp", split_axis=1, concat_axis=1, tiled=True
        ),
        lax.all_to_all(
            slot_gate.reshape(layout + (1,)), "exp", split_axis=1, concat_axis=1, tiled=True
        ),
    )
    grad_gate = jnp.einsum(
        "esd,esf->edf", arrived_inputs, delta_gate, preferred_element_type=jnp.float32
    )
    grad_up = jnp.einsum(
        "esd,esf->edf", arrived_inputs, delta_up, preferred_element_type=jnp.float32
    )
    grad_down = jnp.einsum(
        "esd,esf->edf", scaled, hidden.astype(jnp.bfloat16), preferred_element_type=jnp.float32
    )
    returned_grads = returned_grads.reshape(EXPERTS * capacity, width)
    returned_gate = returned_gate.reshape(EXPERTS * capacity, 1)
    token_grad = jnp.einsum(
        "tc,cd->td", token_place, returned_grads, preferred_element_type=jnp.float32
    ).astype(jnp.bfloat16)
    gate_grad = jnp.einsum(
        "pc,cx->px", placement, returned_gate, preferred_element_type=jnp.float32
    )
    gate_grad = gate_grad.reshape(token_count, 2).astype(jnp.bfloat16)
    reduced = (
        lax.psum_scatter(grad_gate, ("cuts", "fsdp"), scatter_dimension=1, tiled=True),
        lax.psum_scatter(grad_up, ("cuts", "fsdp"), scatter_dimension=1, tiled=True),
        lax.psum_scatter(grad_down, ("cuts", "fsdp"), scatter_dimension=1, tiled=True),
    )
    gradient = jnp.stack([reduced[0], reduced[1], reduced[2]])
    new_params, new_first, new_second = adam_update(params, gradient, moment_first, moment_second)
    return (token_grad, gate_grad, new_params, new_first, new_second)


def solution(mesh):
    return jax.shard_map(
        per_device,
        mesh=mesh,
        in_specs=(
            P(("cuts", "exp", "fsdp"), None),
            P(("cuts", "exp", "fsdp"), None),
            P(("cuts", "exp", "fsdp"), None),
            P(("cuts", "exp", "fsdp"), None),
            P(None, "exp", ("cuts", "fsdp"), None),
            P(None, "exp", ("cuts", "fsdp"), None),
            P(None, "exp", ("cuts", "fsdp"), None),
        ),
        out_specs=(
            P(("cuts", "exp", "fsdp"), None),
            P(("cuts", "exp", "fsdp"), None),
            P(None, "exp", ("cuts", "fsdp"), None),
            P(None, "exp", ("cuts", "fsdp"), None),
            P(None, "exp", ("cuts", "fsdp"), None),
        ),
        check_vma=False,
    )
```

profile of v0, /device:TPU:0, one launch (start us, length us, event | category | flops | bytes accessed | tf_op | source)
XLA Modules:
  0.0 720.5 jit_solution(18314282270735941708)
XLA Ops:
  7.2 3.3 convert_element_type.82
  13.2 4.3 all-to-all-start
  21.2 3.9 all-to-all-start.2
  25.1 2.1 convolution_convert_fusion.1
  29.0 26.4 %all-to-all-done.2 = bf16[4,2,40,4096]{3,2,0,1:T(8,128)(2,1)S(1)} async-done(((bf16[4,2,40,4096]{3,2,0,1:T(8,128)(2,1)}), bf16[4,2,40,4096]{3,2,0,1:T(8,128)(2,1)S(1)}, u32[]{:S(2)}, u32[]{:S(2)}) %all-to-all-start.2) | async-done | bytes 2621472 | tf_op jit(solution)/shard_map/all_to_all | solution.py:53
  55.4 5.1 all-to-all-start.1
  62.6 27.5 %all-to-all-done.1 = bf16[4,2,40,4096]{3,2,0,1:T(8,128)(2,1)} async-done(((bf16[4,2,40,4096]{3,2,0,1:T(8,128)(2,1)}), bf16[4,2,40,4096]{3,2,0,1:T(8,128)(2,1)}, u32[]{:S(2)}, u32[]{:S(2)}) %all-to-all-start.1) | async-done | bytes 2621472 | tf_op jit(solution)/shard_map/all_to_all | solution.py:56
  90.1 3.6 copy.76
  93.7 55.5 %all-gather.2.cloned.1.call-done = bf16[3,4,4096,256]{3,2,1,0:T(8,128)(2,1)} async-done(((bf16[3,4,256,256]{3,2,1,0:T(8,128)(2,1)}), bf16[3,4,4096,256]{3,2,1,0:T(8,128)(2,1)}) %all-gather.2.cloned.1.call-update) | async-done | bytes 25165840 | tf_op jit(solution)/shard_map/all_gather | solution.py:30
  149.2 4.9 fusion.4
  154.1 5.1 fusion.2
  159.2 8.2 %fusion.8 = f32[4,4096,256]{2,1,0:T(8,128)} fusion(bf16[4,80,4096]{2,1,0:T(8,128)(2,1)S(1)} %bitcast.70, f32[4,80]{1,0:T(4,128)S(1)} %reshape.181, f32[4,80,256]{2,1,0:T(8,128)S(1)} %fusion.2, f32[4,80,256]{2,1,0:T(8,128)S(1)} %fusion.4), kind=kOutput, calls=%fused_computation.19 | convolution fusion | flops 675512320 | bytes 20055296 | tf_op jit(solution)/shard_map/esd,esf->edf/dot_general | solution.py:105
  167.7 5.8 multiply_reduce_fusion
  173.5 11.5 %fusion.36 = f32[4,4096,256]{2,1,0:T(8,128)} fusion(bf16[4,80,4096]{2,1,0:T(8,128)(2,1)S(1)} %bitcast.65, bf16[4,80,256]{2,1,0:T(8,128)(2,1)S(1)} %get-tuple-element.9), kind=kOutput, calls=%fused_computation.69 | convolution fusion | flops 671088640 | bytes 19562496 | tf_op jit(solution)/shard_map/esd,esf->edf/dot_general | solution.py:99
  185.1 10.6 %fusion.37 = f32[4,4096,256]{2,1,0:T(8,128)} fusion(bf16[4,80,4096]{2,1,0:T(8,128)(2,1)S(1)} %bitcast.66, bf16[4,80,256]{2,1,0:T(8,128)(2,1)S(1)} %get-tuple-element.10), kind=kOutput, calls=%fused_computation.70 | convolution fusion | flops 671088640 | bytes 19562496 | tf_op jit(solution)/shard_map/esd,esf->edf/dot_general | solution.py:102
  196.3 3.2 all-to-all-start.4
  199.6 6.0 fusion.1
  205.6 6.1 fusion.6
  213.3 3.9 all-to-all-start.3
  218.0 30.4 %all-to-all-done.3 = bf16[4,2,40,4096]{3,2,0,1:T(8,128)(2,1)S(1)} async-done(((bf16[4,2,40,4096]{3,2,0,1:T(8,128)(2,1)}), bf16[4,2,40,4096]{3,2,0,1:T(8,128)(2,1)S(1)}, u32[]{:S(2)}, u32[]{:S(2)}) %all-to-all-start.3) | async-done | bytes 2621472 | tf_op jit(solution)/shard_map/all_to_all | solution.py:92
  250.3 94.5 %reduce-scatter.8.cloned.1.call-done = f32[4,256,256]{2,1,0:T(8,128)} async-done(((f32[4,4096,256]{2,1,0:T(8,128)}), f32[4,256,256]{2,1,0:T(8,128)}) %reduce-scatter.8.cloned.1.call-update) | async-done | bytes 1048592 | tf_op jit(solution)/shard_map/reduce_scatter | solution.py:120
  344.8 180.6 %reduce-scatter.4.cloned.1.call-done = f32[4,256,256]{2,1,0:T(8,128)} async-done(((f32[4,4096,256]{2,1,0:T(8,128)}), f32[4,256,256]{2,1,0:T(8,128)}) %reduce-scatter.4.cloned.1.call-update) | async-done | bytes 1048592 | tf_op jit(solution)/shard_map/reduce_scatter | solution.py:118
  525.4 180.5 %reduce-scatter.6.cloned.1.call-done = f32[4,256,256]{2,1,0:T(8,128)} async-done(((f32[4,4096,256]{2,1,0:T(8,128)}), f32[4,256,256]{2,1,0:T(8,128)}) %reduce-scatter.6.cloned.1.call-update) | async-done | bytes 1048592 | tf_op jit(solution)/shard_map/reduce_scatter | solution.py:119
  705.9 8.0 %multiply_subtract_fusion = (f32[3,4,256,256]{3,2,1,0:T(8,128)}, f32[3,4,256,256]{3,2,1,0:T(8,128)}, f32[3,4,256,256]{3,2,1,0:T(8,128)}) fusion(f32[3,4,256,256]{3,2,1,0:T(8,128)} %param.11, f32[1,4,256,256]{3,2,1,0:T(8,128)} %bitcast.73, f32[1,4,256,256]{3,2,1,0:T(8,128)} %bitcast.75, f32[1,4,256,256]{3,2,1,0:T(8,128)} %bitcast.74, ...), kind=kLoop, calls=%fused_computation.17 | loop fusion | flops 13369344 | bytes 22020096 | tf_op jit(solution)/shard_map/sub | solution.py:20
  (60 shorter events, 15.6 us)
Async XLA Ops:
  7.2 10.8 %copy-start = (bf16[128,4096]{1,0:T(8,128)(2,1)S(1)}, bf16[128,4096]{1,0:T(8,128)(2,1)}, u32[]{:S(2)}) copy-start(bf16[128,4096]{1,0:T(8,128)(2,1)} %param.7) | copy-start | bytes 3145732
  7.2 3.4 copy-start.5
  7.2 3.8 copy-start.6
  7.2 142.0 %all-gather.2.cloned.1.call-start = ((), (), s32[]{:S(2)}) async-start(), calls=%async_computation.8 | async-start | bytes 26738688 | tf_op jit(solution)/shard_map/all_gather | solution.py:30
  13.2 8.0 %all-to-all-start = ((bf16[4,2,40,1]{2,0,3,1:T(4,128)(2,1)}), bf16[4,2,40,1]{2,0,3,1:T(4,128)(2,1)S(1)}, u32[]{:S(2)}, u32[]{:S(2)}) async-start(bf16[4,2,40,1]{2,0,3,1:T(4,128)(2,1)} %copy.73), calls=%async_computation | async-start | bytes 4096 | tf_op jit(solution)/shard_map/all_to_all | solution.py:59
  21.2 34.2 %all-to-all-start.2 = ((bf16[4,2,40,4096]{3,2,0,1:T(8,128)(2,1)}), bf16[4,2,40,4096]{3,2,0,1:T(8,128)(2,1)S(1)}, u32[]{:S(2)}, u32[]{:S(2)}) async-start(bf16[4,2,40,4096]{3,2,0,1:T(8,128)(2,1)} %copy.77), calls=%async_computation.2 | async-start | bytes 5242880 | tf_op jit(solution)/shard_map/all_to_all | solution.py:53
  55.4 5.2 copy-start.3
  55.4 34.7 %all-to-all-start.1 = ((bf16[4,2,40,4096]{3,2,0,1:T(8,128)(2,1)}), bf16[4,2,40,4096]{3,2,0,1:T(8,128)(2,1)}, u32[]{:S(2)}, u32[]{:S(2)}) async-start(bf16[4,2,40,4096]{3,2,0,1:T(8,128)(2,1)} %copy.75), calls=%async_computation.1 | async-start | bytes 5242880 | tf_op jit(solution)/shard_map/all_to_all | solution.py:56
  60.5 284.4 %reduce-scatter.8.cloned.1.call-start = ((), (), s32[]{:S(2)}) async-start(), calls=%async_computation.11 | async-start | bytes 17825792 | tf_op jit(solution)/shard_map/reduce_scatter | solution.py:120
  154.1 5.1 copy-start.2
  159.2 8.2 %copy-start.4 = (f32[4,80,256]{2,1,0:T(8,128)}, f32[4,80,256]{2,1,0:T(8,128)S(1)}, u32[]{:S(2)}) copy-start(f32[4,80,256]{2,1,0:T(8,128)S(1)} %fusion.2) | copy-start | bytes 983044
  167.4 358.0 %reduce-scatter.4.cloned.1.call-start = ((), (), s32[]{:S(2)}) async-start(), calls=%async_computation.9 | async-start | bytes 17825792 | tf_op jit(solution)/shard_map/reduce_scatter | solution.py:118
  185.0 520.9 %reduce-scatter.6.cloned.1.call-start = ((), (), s32[]{:S(2)}) async-start(), calls=%async_computation.10 | async-start | bytes 17825792 | tf_op jit(solution)/shard_map/reduce_scatter | solution.py:119
  196.3 17.0 %all-to-all-start.4 = ((bf16[4,2,40,1]{2,0,3,1:T(4,128)(2,1)}), bf16[4,2,40,1]{2,0,3,1:T(4,128)(2,1)S(1)}, u32[]{:S(2)}, u32[]{:S(2)}) async-start(bf16[4,2,40,1]{2,0,3,1:T(4,128)(2,1)} %copy.82), calls=%async_computation.4 | async-start | bytes 4096 | tf_op jit(solution)/shard_map/all_to_all | solution.py:95
  213.3 35.1 %all-to-all-start.3 = ((bf16[4,2,40,4096]{3,2,0,1:T(8,128)(2,1)}), bf16[4,2,40,4096]{3,2,0,1:T(8,128)(2,1)S(1)}, u32[]{:S(2)}, u32[]{:S(2)}) async-start(bf16[4,2,40,4096]{3,2,0,1:T(8,128)(2,1)} %copy.79), calls=%async_computation.3 | async-start | bytes 5242880 | tf_op jit(solution)/shard_map/all_to_all | solution.py:92
  705.9 8.0 %copy-start.1 = (bf16[128,4096]{1,0:T(8,128)(2,1)S(1)}, bf16[128,4096]{1,0:T(8,128)(2,1)}, u32[]{:S(2)}) copy-start(bf16[128,4096]{1,0:T(8,128)(2,1)} %param.7) | copy-start | bytes 3145732
Sparse Core Ops, SparseCore 0:
  10.7 138.4 all-gather.1
  167.5 177.2 reduce-scatter.7
  349.0 176.4 reduce-scatter.3
  529.4 176.4 reduce-scatter.5
where the time goes:
time: 721 us; the launch traced here: 720 us
  waiting for transfers between devices  596 us (83%)
  matrix products  63.2 us (9%)
  starting transfers between devices  20.6 us (3%)
  between operations  14 us (2%)
  local copies, waits for them, and re-layouts  13.7 us (2%)
  other arithmetic  12.7 us (2%)
    reduce_scatter x1, waiting for transfers between devices, per_device(): lax.psum_scatter(grad_gate, ('cuts', 'fsdp'), scatter_dimension=1, tiled=...  181 us
    reduce_scatter x1, waiting for transfers between devices, per_device(): lax.psum_scatter(grad_up, ('cuts', 'fsdp'), scatter_dimension=1, tiled=True)  180 us
    reduce_scatter x1, waiting for transfers between devices, per_device(): lax.psum_scatter(grad_down, ('cuts', 'fsdp'), scatter_dimension=1, tiled=...  94.5 us
    all_gather x1, waiting for transfers between devices, per_device(): lax.all_gather(params.astype(jnp.bfloat16), ('cuts', 'fsdp'), axis=2, til...  55.5 us
    all_to_all x1, waiting for transfers between devices, per_device(): lax.all_to_all(slot_grads.reshape(layout + (width,)), 'exp', split_axis=1...  30.4 us
    all_to_all x1, waiting for transfers between devices, per_device(): lax.all_to_all(send_upstream.reshape(layout + (width,)), 'exp', split_axi...  27.5 us
    all_to_all x1, waiting for transfers between devices, per_device(): lax.all_to_all(send_inputs.reshape(layout + (width,)), 'exp', split_axis=...  26.4 us
  transfers between devices with their start and end apart: 9, of which 8 were waited for; matrix products, arithmetic and copies ran while one was open for 8% of the time, Pallas kernels for 0%

commit v1 on v0

--- a/solution.py
+++ b/solution.py
@@ -2,6 +2,7 @@
 import jax.numpy as jnp
 from jax import lax
 from jax.sharding import PartitionSpec as P
+from jax.lax import all_gather
 
 EXPERTS = 8
 decay_first = 0.9
@@ -27,7 +28,8 @@
     local_count = params.shape[1]
     exp_count = lax.axis_size("exp")
     capacity = 10 * token_count // 32
-    weights = lax.all_gather(params.astype(jnp.bfloat16), ("cuts", "fsdp"), axis=2, tiled=True)
+    q_in = params.astype(jnp.bfloat16)
+    weights = jnp.concatenate(all_gather(q_in, ("cuts", "fsdp")), 2)
     flat_ids = expert_ids.reshape(-1)
     onehot = (flat_ids[:, None] == jnp.arange(EXPERTS, dtype=jnp.int32)[None, :]).astype(jnp.int32)
     before = jnp.cumsum(onehot, axis=0) - onehot

time: 721 us -> 751 us (1.042)
  local copies, waits for them, and re-layouts: 13.7 us -> 53.9 us
    all_gather x0 -> x1, local copies, waits for them, and re-layouts: none -> 20.7 us  [per_device(): weights = jnp.concatenate(all_gather(q_in, ('cuts', 'fsdp')), 2)]
    slice x1 -> x2, local copies, waits for them, and re-layouts: 0.21 us -> 12.4 us  [the longest x1 12.2 us: per_device(): w_down = weights[2]]
  transfers between devices with their start and end apart: 9 -> 9, of which waited for: 8 -> 8; matrix products, arithmetic and copies ran while one was open for 8% -> 9% of each run, Pallas kernels for 0% -> 0%
where the time goes in v1:
time: 751 us; the launch traced here: 750 us
  waiting for transfers between devices  590 us (79%)
  matrix products  56.5 us (8%)
  local copies, waits for them, and re-layouts  53.9 us (7%)
  starting transfers between devices  22.9 us (3%)
  between operations  14 us (2%)
  other arithmetic  12.7 us (2%)
    reduce_scatter x1, waiting for transfers between devices, per_device(): lax.psum_scatter(grad_gate, ('cuts', 'fsdp'), scatter_dimension=1, tiled=...  181 us
    reduce_scatter x1, waiting for transfers between devices, per_device(): lax.psum_scatter(grad_up, ('cuts', 'fsdp'), scatter_dimension=1, tiled=True)  180 us
    reduce_scatter x1, waiting for transfers between devices, per_device(): lax.psum_scatter(grad_down, ('cuts', 'fsdp'), scatter_dimension=1, tiled=...  90 us
    all_gather x1, waiting for transfers between devices, per_device(): weights = jnp.concatenate(all_gather(q_in, ('cuts', 'fsdp')), 2)  53.9 us
    all_to_all x1, waiting for transfers between devices, per_device(): lax.all_to_all(slot_grads.reshape(layout + (width,)), 'exp', split_axis=1...  30.5 us
    all_to_all x1, waiting for transfers between devices, per_device(): lax.all_to_all(send_inputs.reshape(layout + (width,)), 'exp', split_axis=...  28 us
    all_to_all x1, waiting for transfers between devices, per_device(): lax.all_to_all(send_upstream.reshape(layout + (width,)), 'exp', split_axi...  26 us
    all_gather x1, local copies, waits for them, and re-layouts, per_device(): weights = jnp.concatenate(all_gather(q_in, ('cuts', 'fsdp')), 2)  20.7 us
  transfers between devices with their start and end apart: 9, of which 8 were waited for; matrix products, arithmetic and copies ran while one was open for 9% of the time, Pallas kernels for 0%

profile of v1, /device:TPU:0, one launch (start us, length us, event | category | flops | bytes accessed | tf_op | source)
XLA Modules:
  0.0 750.0 jit_solution(3681823673578046628)
XLA Ops:
  7.2 3.3 convert_element_type.82
  13.2 4.3 all-to-all-start
  21.2 5.0 all-to-all-start.2
  28.9 28.0 %all-to-all-done.2 = bf16[4,2,40,4096]{3,2,0,1:T(8,128)(2,1)} async-done(((bf16[4,2,40,4096]{3,2,0,1:T(8,128)(2,1)}), bf16[4,2,40,4096]{3,2,0,1:T(8,128)(2,1)}, u32[]{:S(2)}, u32[]{:S(2)}) %all-to-all-start.2) | async-done | bytes 2621472 | tf_op jit(solution)/shard_map/all_to_all | solution.py:55
  56.8 5.1 all-to-all-start.1
  62.1 3.6 copy.83
  65.7 26.0 %all-to-all-done.1 = bf16[4,2,40,4096]{3,2,0,1:T(8,128)(2,1)} async-done(((bf16[4,2,40,4096]{3,2,0,1:T(8,128)(2,1)}), bf16[4,2,40,4096]{3,2,0,1:T(8,128)(2,1)}, u32[]{:S(2)}, u32[]{:S(2)}) %all-to-all-start.1) | async-done | bytes 2621472 | tf_op jit(solution)/shard_map/all_to_all | solution.py:58
  91.7 3.6 copy.80
  95.3 53.9 %all-gather.3.cloned.1.call-done = bf16[48,4,256,256]{3,2,1,0:T(8,128)(2,1)} async-done(((bf16[3,4,256,256]{3,2,1,0:T(8,128)(2,1)}), bf16[48,4,256,256]{3,2,1,0:T(8,128)(2,1)}) %all-gather.3.cloned.1.call-update) | async-done | bytes 25165840 | tf_op jit(solution)/shard_map/all_gather | solution.py:32
  149.2 20.7 %copy.94 = bf16[16,3,4,256,256]{4,3,0,2,1:T(8,128)(2,1)} copy(bf16[16,3,4,256,256]{4,3,2,1,0:T(8,128)(2,1)} %bitcast.70) | data formatting | bytes 50331648 | tf_op jit(solution)/shard_map/all_gather | solution.py:32
  169.8 12.2 %fusion.30 = (bf16[1,4,16,256,256]{4,3,2,1,0:T(8,128)(2,1)}, bf16[1,4,16,256,256]{4,3,2,1,0:T(8,128)(2,1)S(1)}, bf16[1,4,16,256,256]{4,3,2,1,0:T(8,128)(2,1)S(1)}) fusion(bf16[3,4,16,256,256]{4,3,2,1,0:T(8,128)(2,1)} %bitcast.60), kind=kLoop, calls=%fused_computation.62 | loop fusion | bytes 50331648 | tf_op jit(solution)/shard_map/slice | solution.py:71
  188.8 8.2 %fusion.2 = f32[4,4096,256]{2,1,0:T(8,128)} fusion(bf16[4,80,4096]{2,1,0:T(8,128)(2,1)S(1)} %bitcast.69, f32[4,80]{1,0:T(4,128)S(1)} %reshape.192, f32[4,80,256]{2,1,0:T(8,128)S(1)} %fusion.31, f32[4,80,256]{2,1,0:T(8,128)S(1)} %fusion.32), kind=kOutput, calls=%fused_computation.12 | convolution fusion | flops 675512320 | bytes 20055296 | tf_op jit(solution)/shard_map/esd,esf->edf/dot_general | solution.py:107
  197.2 6.0 multiply_reduce_fusion
  203.3 11.4 %fusion.34 = f32[4,4096,256]{2,1,0:T(8,128)} fusion(bf16[4,80,4096]{2,1,0:T(8,128)(2,1)S(1)} %bitcast.64, bf16[4,80,256]{2,1,0:T(8,128)(2,1)S(1)} %get-tuple-element.12), kind=kOutput, calls=%fused_computation.66 | convolution fusion | flops 671088640 | bytes 19562496 | tf_op jit(solution)/shard_map/esd,esf->edf/dot_general | solution.py:101
  214.7 11.9 %fusion.35 = f32[4,4096,256]{2,1,0:T(8,128)} fusion(bf16[4,80,4096]{2,1,0:T(8,128)(2,1)} %bitcast.61, bf16[4,80,256]{2,1,0:T(8,128)(2,1)S(1)} %get-tuple-element.13), kind=kOutput, calls=%fused_computation.67 | convolution fusion | flops 671088640 | bytes 19562496 | tf_op jit(solution)/shard_map/esd,esf->edf/dot_general | solution.py:104
  227.4 3.2 all-to-all-start.4
  230.6 6.0 fusion.33
  236.6 6.1 fusion
  244.3 5.0 all-to-all-start.3
  250.1 30.5 %all-to-all-done.3 = bf16[4,2,40,4096]{3,2,0,1:T(8,128)(2,1)} async-done(((bf16[4,2,40,4096]{3,2,0,1:T(8,128)(2,1)}), bf16[4,2,40,4096]{3,2,0,1:T(8,128)(2,1)}, u32[]{:S(2)}, u32[]{:S(2)}) %all-to-all-start.3) | async-done | bytes 2621472 | tf_op jit(solution)/shard_map/all_to_all | solution.py:94
  284.5 90.0 %reduce-scatter.8.cloned.1.call-done = f32[4,256,256]{2,1,0:T(8,128)} async-done(((f32[4,4096,256]{2,1,0:T(8,128)}), f32[4,256,256]{2,1,0:T(8,128)}) %reduce-scatter.8.cloned.1.call-update) | async-done | bytes 1048592 | tf_op jit(solution)/shard_map/reduce_scatter | solution.py:122
  374.4 180.6 %reduce-scatter.4.cloned.1.call-done = f32[4,256,256]{2,1,0:T(8,128)} async-done(((f32[4,4096,256]{2,1,0:T(8,128)}), f32[4,256,256]{2,1,0:T(8,128)}) %reduce-scatter.4.cloned.1.call-update) | async-done | bytes 1048592 | tf_op jit(solution)/shard_map/reduce_scatter | solution.py:120
  555.0 180.4 %reduce-scatter.6.cloned.1.call-done = f32[4,256,256]{2,1,0:T(8,128)} async-done(((f32[4,4096,256]{2,1,0:T(8,128)}), f32[4,256,256]{2,1,0:T(8,128)}) %reduce-scatter.6.cloned.1.call-update) | async-done | bytes 1048592 | tf_op jit(solution)/shard_map/reduce_scatter | solution.py:121
  735.4 8.0 %multiply_subtract_fusion = (f32[3,4,256,256]{3,2,1,0:T(8,128)}, f32[3,4,256,256]{3,2,1,0:T(8,128)}, f32[3,4,256,256]{3,2,1,0:T(8,128)}) fusion(f32[3,4,256,256]{3,2,1,0:T(8,128)} %param.11, f32[1,4,256,256]{3,2,1,0:T(8,128)} %bitcast.75, f32[1,4,256,256]{3,2,1,0:T(8,128)} %bitcast.77, f32[1,4,256,256]{3,2,1,0:T(8,128)} %bitcast.76, ...), kind=kLoop, calls=%fused_computation.10 | loop fusion | flops 13369344 | bytes 22020096 | tf_op jit(solution)/shard_map/sub | solution.py:21
  (68 shorter events, 23.1 us)
Async XLA Ops:
  7.2 10.8 %copy-start = (bf16[128,4096]{1,0:T(8,128)(2,1)S(1)}, bf16[128,4096]{1,0:T(8,128)(2,1)}, u32[]{:S(2)}) copy-start(bf16[128,4096]{1,0:T(8,128)(2,1)} %param.7) | copy-start | bytes 3145732
  7.2 3.4 copy-start.8
  7.2 3.8 copy-start.9
  7.2 142.0 %all-gather.3.cloned.1.call-start = ((), (), s32[]{:S(2)}) async-start(), calls=%async_computation.11 | async-start | bytes 26738688 | tf_op jit(solution)/shard_map/all_gather | solution.py:32
  13.2 8.0 %all-to-all-start = ((bf16[4,2,40,1]{2,0,3,1:T(4,128)(2,1)}), bf16[4,2,40,1]{2,0,3,1:T(4,128)(2,1)S(1)}, u32[]{:S(2)}, u32[]{:S(2)}) async-start(bf16[4,2,40,1]{2,0,3,1:T(4,128)(2,1)} %copy.77), calls=%async_computation | async-start | bytes 4096 | tf_op jit(solution)/shard_map/all_to_all | solution.py:61
  20.6 5.6 copy-start.7
  21.2 35.6 %all-to-all-start.2 = ((bf16[4,2,40,4096]{3,2,0,1:T(8,128)(2,1)}), bf16[4,2,40,4096]{3,2,0,1:T(8,128)(2,1)}, u32[]{:S(2)}, u32[]{:S(2)}) async-start(bf16[4,2,40,4096]{3,2,0,1:T(8,128)(2,1)} %copy.82), calls=%async_computation.2 | async-start | bytes 5242880 | tf_op jit(solution)/shard_map/all_to_all | solution.py:55
  56.8 34.9 %all-to-all-start.1 = ((bf16[4,2,40,4096]{3,2,0,1:T(8,128)(2,1)}), bf16[4,2,40,4096]{3,2,0,1:T(8,128)(2,1)}, u32[]{:S(2)}, u32[]{:S(2)}) async-start(bf16[4,2,40,4096]{3,2,0,1:T(8,128)(2,1)} %copy.79), calls=%async_computation.1 | async-start | bytes 5242880 | tf_op jit(solution)/shard_map/all_to_all | solution.py:58
  61.9 312.5 %reduce-scatter.8.cloned.1.call-start = ((), (), s32[]{:S(2)}) async-start(), calls=%async_computation.10 | async-start | bytes 17825792 | tf_op jit(solution)/shard_map/reduce_scatter | solution.py:122
  169.8 12.2 %copy-start.3 = (bf16[4,2,40,4096]{3,2,1,0:T(8,128)(2,1)S(1)}, bf16[4,2,40,4096]{3,2,1,0:T(8,128)(2,1)}, u32[]{:S(2)}) copy-start(bf16[4,2,40,4096]{3,2,1,0:T(8,128)(2,1)} %copy.83) | copy-start | bytes 7864324
  182.0 3.2 copy-start.2
  182.0 6.3 copy-start.5
  185.2 3.6 copy-start.6
  197.0 358.0 %reduce-scatter.4.cloned.1.call-start = ((), (), s32[]{:S(2)}) async-start(), calls=%async_computation.8 | async-start | bytes 17825792 | tf_op jit(solution)/shard_map/reduce_scatter | solution.py:120
  197.2 6.0 copy-start.4
  214.7 520.7 %reduce-scatter.6.cloned.1.call-start = ((), (), s32[]{:S(2)}) async-start(), calls=%async_computation.9 | async-start | bytes 17825792 | tf_op jit(solution)/shard_map/reduce_scatter | solution.py:121
  227.4 17.0 %all-to-all-start.4 = ((bf16[4,2,40,1]{2,0,3,1:T(4,128)(2,1)}), bf16[4,2,40,1]{2,0,3,1:T(4,128)(2,1)S(1)}, u32[]{:S(2)}, u32[]{:S(2)}) async-start(bf16[4,2,40,1]{2,0,3,1:T(4,128)(2,1)} %copy.87), calls=%async_computation.4 | async-start | bytes 4096 | tf_op jit(solution)/shard_map/all_to_all | solution.py:97
  244.3 36.3 %all-to-all-start.3 = ((bf16[4,2,40,4096]{3,2,0,1:T(8,128)(2,1)}), bf16[4,2,40,4096]{3,2,0,1:T(8,128)(2,1)}, u32[]{:S(2)}, u32[]{:S(2)}) async-start(bf16[4,2,40,4096]{3,2,0,1:T(8,128)(2,1)} %copy.84), calls=%async_computation.3 | async-start | bytes 5242880 | tf_op jit(solution)/shard_map/all_to_all | solution.py:94
  735.4 8.0 %copy-start.1 = (bf16[128,4096]{1,0:T(8,128)(2,1)S(1)}, bf16[128,4096]{1,0:T(8,128)(2,1)}, u32[]{:S(2)}) copy-start(bf16[128,4096]{1,0:T(8,128)(2,1)} %param.7) | copy-start | bytes 3145732
Sparse Core Ops, SparseCore 0:
  10.7 138.4 all-gather.2
  197.1 177.2 reduce-scatter.7
  378.6 176.3 reduce-scatter.3
  559.0 176.4 reduce-scatter.5
